TPU v7x, 256 devices: a whole 4x4x8 slice. The times are simulated.
256 devices in a mesh: dp: 8 (over x, core), fsdp: 8 (over z), mp: 4 (over y).
Axes of the slice: x: 4, y: 4, z: 8, core: 2. Of those that a mesh axis runs over, the one named last changes fastest.
Arguments:
- gradients: bfloat16 [64, 12, 2, 256, 1024], P(('dp', 'fsdp'), None, None, None, 'mp'), may hold values from -16 to 16
- master: float32 [12, 2, 256, 1024], P(None, None, ('dp', 'fsdp'), 'mp'), may hold values from -0.375 to 0.375
- teacher: float32 [12, 2, 256, 1024], P(None, None, ('dp', 'fsdp'), 'mp'), may hold values from -0.375 to 0.375
- first_moment: float32 [12, 2, 256, 1024], P(None, None, ('dp', 'fsdp'), 'mp'), may hold values from -2.2888184e-05 to 2.2888184e-05
- second_moment: float32 [12, 2, 256, 1024], P(None, None, ('dp', 'fsdp'), 'mp'), may hold values from 0 to 1, as said below
- layer_rates: float32 [12], replicated, may hold values from 0.02 to 0.2
Outputs:
- master_new: float32 [12, 2, 256, 1024], P(None, None, ('dp', 'fsdp'), 'mp')
- teacher_new: float32 [12, 2, 256, 1024], P(None, None, ('dp', 'fsdp'), 'mp')
- first_new: float32 [12, 2, 256, 1024], P(None, None, ('dp', 'fsdp'), 'mp')
- second_new: float32 [12, 2, 256, 1024], P(None, None, ('dp', 'fsdp'), 'mp')
- student_weights: bfloat16 [12, 2, 256, 1024], P(None, None, None, 'mp')
- teacher_weights: bfloat16 [12, 2, 256, 1024], P(None, None, None, 'mp')
Inputs may be any that keep to these rules, and one draw needn't show every extreme that they name: `second_moment`: every entry is positive.
All inputs are finite; a program needn't handle non-finite values.
Results may differ from a plain program's by a relative error of at most 0.0004.
Values may be sent and summed in bfloat16 or wider, within the bound.
No kernel may reach another device: no remote copies, remote signals or barrier semaphores. Data moves between devices by JAX's collectives and lax.ppermute only.
A program may use at most 64 MiB of HBM per device.

v0:
```python
import jax
import jax.numpy as jnp
from jax import lax
from jax.sharding import PartitionSpec as P

OWN = ("dp", "fsdp")
ALL = ("dp", "fsdp", "mp")
CLIP_NORM = 0.1
BETA_ONE = 0.9
BETA_TWO = 0.999
BIAS_ONE = 1.0 - 0.9**50 * 0.9**50
BIAS_TWO = 1.0 - 0.999**50 * 0.999**50
ADAM_EPS = 1e-08
DECAY = 0.05
EMA_KEEP = 0.95


def shards(gradients, master, teacher, first_moment, second_moment, layer_rates):
    own_grad = gradients[0].astype(jnp.float32)
    summed = lax.psum_scatter(own_grad, OWN, scatter_dimension=2, tiled=True)
    mean_grad = summed / 64.0
    norm_sq = lax.psum(jnp.sum(mean_grad * mean_grad), ALL)
    clip_factor = jnp.minimum(1.0, CLIP_NORM / (jnp.sqrt(norm_sq) + 1e-06))
    clipped = clip_factor * mean_grad
    first_new = BETA_ONE * first_moment + (1.0 - BETA_ONE) * clipped
    second_new = BETA_TWO * second_moment + (1.0 - BETA_TWO) * clipped * clipped
    direction = first_new / BIAS_ONE / (jnp.sqrt(second_new / BIAS_TWO) + ADAM_EPS) + DECAY * master
    layer_rate = layer_rates[:, None, None, None]
    master_new = master - layer_rate * direction
    teacher_new = EMA_KEEP * teacher + (1.0 - EMA_KEEP) * master_new
    student = lax.all_gather(master_new.astype(jnp.bfloat16), OWN, axis=2, tiled=True)
    teach = lax.all_gather(teacher_new.astype(jnp.bfloat16), OWN, axis=2, tiled=True)
    return (master_new, teacher_new, first_new, second_new, student, teach)


def solution(mesh):
    own = P(None, None, OWN, "mp")
    gathered = P(None, None, None, "mp")
    in_specs = (P(OWN, None, None, None, "mp"), own, own, own, own, P())
    out_specs = (own, own, own, own, gathered, gathered)
    return jax.shard_map(shards, mesh=mesh, in_specs=in_specs, out_specs=out_specs, check_vma=False)
```

profile of v0, /device:TPU:1, one launch (start us, length us, event | category | flops | bytes accessed | tf_op | source)
XLA Modules:
  0.0 413.0 jit_solution(480780248336302537)
XLA Ops:
  7.2 0.0 reduce-scatter.2.cloned.1.call-start
  7.2 7.0 %bitcast_convert_fusion = f32[12,2,256,256]{3,0,1,2:T(8,128)} fusion(bf16[1,12,2,256,256]{4,3,2,1,0:T(8,128)(2,1)} %param.6), kind=kLoop, calls=%fused_computation | loop fusion | flops 1572864 | bytes 9437184 | tf_op jit(solution)/shard_map/convert_element_type | solution.py:19
  14.2 0.0 copy-start
  14.2 0.0 copy-start.1
  14.2 0.0 copy-start.2
  14.2 0.0 copy-start.3
  14.2 0.0 copy-start.4
  14.2 0.0 reduce-scatter.2.cloned.1.call-update
  14.3 0.0 all-gather.3.cloned.1.call-start
  14.3 151.8 %reduce-scatter.2.cloned.1.call-done = f32[12,2,4,256]{3,0,1,2:T(8,128)} async-done(((f32[12,2,256,256]{3,0,1,2:T(8,128)}), f32[12,2,4,256]{3,0,1,2:T(8,128)}) %reduce-scatter.2.cloned.1.call-update) | async-done | bytes 98320 | tf_op jit(solution)/shard_map/reduce_scatter | solution.py:20
  166.1 1.5 multiply_reduce_fusion
  167.6 78.7 %psum.7 = f32[]{:T(128)} all-reduce(f32[]{:T(128)} %multiply_reduce_fusion), channel_id=1, replica_groups=mesh['dp'=8,'fsdp'=8,'mp'=4] {'dp','fsdp','mp'}, use_global_device_ids=true, to_apply=%region_2.0 | all-reduce | flops 1 | bytes 8 | tf_op jit(solution)/shard_map/psum | solution.py:22
  247.1 0.0 copy-done
  247.1 0.0 copy-done.1
  247.1 0.0 copy-done.2
  247.1 0.0 copy-done.3
  247.1 0.0 copy-done.4
  247.1 1.1 fusion.5
  248.3 0.7 copy.18
  248.9 0.0 all-gather.3.cloned.1.call-update
  249.0 0.0 all-gather.5.cloned.1.call-start
  249.0 0.7 copy.19
  249.7 0.0 all-gather.5.cloned.1.call-update
  249.7 0.7 copy.20
  250.4 0.7 copy.21
  251.1 0.7 copy.22
  251.8 0.7 copy.23
  252.5 71.5 %all-gather.3.cloned.1.call-done = bf16[12,2,256,256]{3,1,0,2:T(2,128)(2,1)} async-done(((bf16[12,2,4,256]{3,1,0,2:T(2,128)(2,1)}), bf16[12,2,256,256]{3,1,0,2:T(2,128)(2,1)}) %all-gather.3.cloned.1.call-update) | async-done | bytes 3145744 | tf_op jit(solution)/shard_map/all_gather | solution.py:31
  324.1 4.3 %copy.24 = bf16[12,2,256,256]{3,2,1,0:T(8,128)(2,1)} copy(bf16[12,2,256,256]{3,1,0,2:T(2,128)(2,1)} %all-gather.3.cloned.1.call-done) | data formatting | bytes 6291456
  328.4 73.9 %all-gather.5.cloned.1.call-done = bf16[12,2,256,256]{3,1,0,2:T(2,128)(2,1)} async-done(((bf16[12,2,4,256]{3,1,0,2:T(2,128)(2,1)}), bf16[12,2,256,256]{3,1,0,2:T(2,128)(2,1)}) %all-gather.5.cloned.1.call-update) | async-done | bytes 3145744 | tf_op jit(solution)/shard_map/all_gather | solution.py:32
  402.2 4.3 %copy.25 = bf16[12,2,256,256]{3,2,1,0:T(8,128)(2,1)} copy(bf16[12,2,256,256]{3,1,0,2:T(2,128)(2,1)} %all-gather.5.cloned.1.call-done) | data formatting | bytes 6291456
  (1 shorter events, 0.0 us)
Async XLA Ops:
  7.2 158.9 %reduce-scatter.2.cloned.1.call-start = ((), (), s32[]{:S(2)}) async-start(), calls=%async_computation.1 | async-start | bytes 8519680 | tf_op jit(solution)/shard_map/reduce_scatter | solution.py:20
  14.2 232.9 %copy-start = (f32[12,2,4,256]{3,2,1,0:T(4,128)S(1)}, f32[12,2,4,256]{3,2,1,0:T(4,128)}, u32[]{:S(2)}) copy-start(f32[12,2,4,256]{3,2,1,0:T(4,128)} %param.8) | copy-start | bytes 294916
  14.2 232.9 %copy-start.1 = (f32[12,2,4,256]{3,2,1,0:T(4,128)S(1)}, f32[12,2,4,256]{3,2,1,0:T(4,128)}, u32[]{:S(2)}) copy-start(f32[12,2,4,256]{3,2,1,0:T(4,128)} %param.7) | copy-start | bytes 294916
  14.2 232.9 %copy-start.2 = (f32[12,2,4,256]{3,2,1,0:T(4,128)S(1)}, f32[12,2,4,256]{3,2,1,0:T(4,128)}, u32[]{:S(2)}) copy-start(f32[12,2,4,256]{3,2,1,0:T(4,128)} %param.9) | copy-start | bytes 294916
  14.2 232.9 %copy-start.3 = (f32[12,2,4,256]{3,2,1,0:T(4,128)S(1)}, f32[12,2,4,256]{3,2,1,0:T(4,128)}, u32[]{:S(2)}) copy-start(f32[12,2,4,256]{3,2,1,0:T(4,128)} %param.10) | copy-start | bytes 294916
  14.2 232.9 %copy-start.4 = (f32[12]{0:T(128)S(1)}, f32[12]{0:T(128)}, u32[]{:S(2)}) copy-start(f32[12]{0:T(128)} %param.11) | copy-start | bytes 148
  14.3 309.8 %all-gather.3.cloned.1.call-start = ((), (), s32[]{:S(2)}) async-start(), calls=%async_computation.2 | async-start | bytes 3194880 | tf_op jit(solution)/shard_map/all_gather | solution.py:31
  249.0 153.3 %all-gather.5.cloned.1.call-start = ((), (), s32[]{:S(2)}) async-start(), calls=%async_computation.3 | async-start | bytes 3194880 | tf_op jit(solution)/shard_map/all_gather | solution.py:32
Sparse Core Ops, SparseCore 0:
  14.4 151.6 reduce-scatter.1
  249.1 74.9 all-gather.2
  326.8 75.3 all-gather.4
where the time goes:
time: 413 us
  waiting for transfers between devices  297 us (72%)
  blocking collectives  78.7 us (19%)
  between operations  14.5 us (4%)
  local copies, waits for them, and re-layouts  12.7 us (3%)
  other arithmetic  9.68 us (2%)
    reduce_scatter x1, waiting for transfers between devices, shards(): summed = lax.psum_scatter(own_grad, OWN, scatter_dimension=2, tiled=True)  152 us
    psum x1, blocking collectives, shards(): norm_sq = lax.psum(jnp.sum(mean_grad * mean_grad), ALL)  78.7 us
    all_gather x1, waiting for transfers between devices, shards(): lax.all_gather(teacher_new.astype(jnp.bfloat16), OWN, axis=2, tiled=True)  73.9 us
    all_gather x1, waiting for transfers between devices, shards(): lax.all_gather(master_new.astype(jnp.bfloat16), OWN, axis=2, tiled=True)  71.5 us
    unnamed x16, local copies, waits for them, and re-layouts  11.4 us
  transfers between devices with their start and end apart: 3, of which 3 were waited for; matrix products, arithmetic and copies ran while one was open for 2% of the time, Pallas kernels for 0%

commit v1 on v0

--- a/solution.py
+++ b/solution.py
@@ -29,7 +29,9 @@
     master_new = master - layer_rate * direction
     teacher_new = EMA_KEEP * teacher + (1.0 - EMA_KEEP) * master_new
     student = lax.all_gather(master_new.astype(jnp.bfloat16), OWN, axis=2, tiled=True)
-    teach = lax.all_gather(teacher_new.astype(jnp.bfloat16), OWN, axis=2, tiled=True)
+    array = teacher_new.astype(jnp.bfloat16)
+    copies = jnp.concatenate([array] * lax.axis_size(OWN), axis=2)
+    teach = lax.all_to_all(copies, OWN, 2, 2, tiled=True)
     return (master_new, teacher_new, first_new, second_new, student, teach)
 
 

time: 413 us -> 419 us (1.015)
  waiting for transfers between devices: 297 us -> 254 us
  local copies, waits for them, and re-layouts: 12.7 us -> 52.7 us
  starting transfers between devices: 0.12 us -> 7.85 us
    all_to_all x0 -> x1, waiting for transfers between devices: none -> 102 us  [shards(): teach = lax.all_to_all(copies, OWN, 2, 2, tiled=True)]
    all_gather x1 -> x0, waiting for transfers between devices: 73.9 us -> none  [shards(): lax.all_gather(teacher_new.astype(jnp.bfloat16), OWN, axis=2, tiled=True)]
    all_gather x1, waiting for transfers between devices: 71.5 us -> 0.01 us  [shards(): lax.all_gather(master_new.astype(jnp.bfloat16), OWN, axis=2, tiled=True)]
    unnamed x16 -> x78, local copies, waits for them, and re-layouts: 11.4 us -> 51.4 us
    all_to_all x0 -> x1, starting transfers between devices: none -> 7.77 us  [shards(): teach = lax.all_to_all(copies, OWN, 2, 2, tiled=True)]
  transfers between devices with their start and end apart: 3 -> 3, of which waited for: 3 -> 2; matrix products, arithmetic and copies ran while one was open for 2% -> 2% of each run, Pallas kernels for 0% -> 0%
where the time goes in v1:
time: 419 us; the launch traced here: 418 us
  waiting for transfers between devices  254 us (61%)
  blocking collectives  78.7 us (19%)
  local copies, waits for them, and re-layouts  52.7 us (13%)
  between operations  14.9 us (4%)
  other arithmetic  10.3 us (2%)
  starting transfers between devices  7.85 us (2%)
    reduce_scatter x1, waiting for transfers between devices, shards(): summed = lax.psum_scatter(own_grad, OWN, scatter_dimension=2, tiled=True)  152 us
    all_to_all x1, waiting for transfers between devices, shards(): teach = lax.all_to_all(copies, OWN, 2, 2, tiled=True)  102 us
    psum x1, blocking collectives, shards(): norm_sq = lax.psum(jnp.sum(mean_grad * mean_grad), ALL)  78.7 us
    unnamed x78, local copies, waits for them, and re-layouts  51.4 us
  transfers between devices with their start and end apart: 3, of which 2 were waited for; matrix products, arithmetic and copies ran while one was open for 2% of the time, Pallas kernels for 0%

profile of v1, /device:TPU:1, one launch (start us, length us, event | category | flops | bytes accessed | tf_op | source)
XLA Modules:
  0.0 418.2 jit_solution(8010870523226407238)
XLA Ops:
  7.2 7.0 %bitcast_convert_fusion = f32[12,2,256,256]{3,0,1,2:T(8,128)} fusion(bf16[1,12,2,256,256]{4,3,2,1,0:T(8,128)(2,1)} %param.6), kind=kLoop, calls=%fused_computation | loop fusion | flops 1572864 | bytes 9437184 | tf_op jit(solution)/shard_map/convert_element_type | solution.py:19
  14.3 151.8 %reduce-scatter.2.cloned.1.call-done = f32[12,2,4,256]{3,0,1,2:T(8,128)} async-done(((f32[12,2,256,256]{3,0,1,2:T(8,128)}), f32[12,2,4,256]{3,0,1,2:T(8,128)}) %reduce-scatter.2.cloned.1.call-update) | async-done | bytes 98320 | tf_op jit(solution)/shard_map/reduce_scatter | solution.py:20
  166.1 1.5 multiply_reduce_fusion
  167.6 78.7 %psum.7 = f32[]{:T(128)} all-reduce(f32[]{:T(128)} %multiply_reduce_fusion), channel_id=1, replica_groups=mesh['dp'=8,'fsdp'=8,'mp'=4] {'dp','fsdp','mp'}, use_global_device_ids=true, to_apply=%region_2.0 | all-reduce | flops 1 | bytes 8 | tf_op jit(solution)/shard_map/psum | solution.py:22
  247.1 1.7 constant_dynamic-update-slice_fusion.63
  250.1 0.6 constant_dynamic-update-slice_fusion.60
  251.4 0.6 constant_dynamic-update-slice_fusion.58
  252.0 0.6 constant_dynamic-update-slice_fusion.57
  252.6 0.6 constant_dynamic-update-slice_fusion.56
  254.5 0.6 constant_dynamic-update-slice_fusion.53
  255.1 0.6 constant_dynamic-update-slice_fusion.52
  257.6 0.6 constant_dynamic-update-slice_fusion.48
  259.5 0.6 constant_dynamic-update-slice_fusion.45
  260.1 0.6 constant_dynamic-update-slice_fusion.44
  260.7 0.6 constant_dynamic-update-slice_fusion.43
  261.4 0.6 constant_dynamic-update-slice_fusion.42
  262.6 0.6 constant_dynamic-update-slice_fusion.40
  263.2 0.6 constant_dynamic-update-slice_fusion.39
  263.9 0.6 constant_dynamic-update-slice_fusion.38
  265.1 0.6 constant_dynamic-update-slice_fusion.36
  267.0 0.6 constant_dynamic-update-slice_fusion.33
  268.2 0.6 constant_dynamic-update-slice_fusion.31
  268.9 0.6 constant_dynamic-update-slice_fusion.30
  270.1 0.6 constant_dynamic-update-slice_fusion.28
  270.7 0.6 constant_dynamic-update-slice_fusion.27
  271.4 0.6 constant_dynamic-update-slice_fusion.26
  272.0 0.6 constant_dynamic-update-slice_fusion.25
  272.6 0.6 constant_dynamic-update-slice_fusion.24
  273.2 0.6 constant_dynamic-update-slice_fusion.23
  273.9 0.6 constant_dynamic-update-slice_fusion.22
  274.5 0.6 constant_dynamic-update-slice_fusion.21
  277.0 0.6 constant_dynamic-update-slice_fusion.17
  277.6 0.6 constant_dynamic-update-slice_fusion.16
  278.9 0.6 constant_dynamic-update-slice_fusion.14
  280.7 0.6 constant_dynamic-update-slice_fusion.11
  282.6 0.6 constant_dynamic-update-slice_fusion.8
  286.3 0.6 constant_dynamic-update-slice_fusion.2
  287.0 0.6 constant_dynamic-update-slice_fusion.1
  287.6 0.6 constant_dynamic-update-slice_fusion
  288.2 7.8 %all-to-all-start = ((bf16[12,2,256,256]{3,0,1,2:T(8,128)(2,1)}), bf16[12,2,256,256]{3,0,1,2:T(8,128)(2,1)}, u32[]{:S(2)}, u32[]{:S(2)}) async-start(bf16[12,2,256,256]{3,0,1,2:T(8,128)(2,1)} %constant_dynamic-update-slice_fusion), calls=%async_computation.1 | async-start | bytes 8388608 | tf_op jit(solution)/shard_map/all_to_all | solution.py:34
  296.1 0.7 copy.32
  296.8 0.7 copy.33
  297.5 0.7 copy.34
  298.2 0.7 copy.35
  298.9 0.7 copy.36
  299.6 101.9 %all-to-all-done = bf16[12,2,256,256]{3,0,1,2:T(8,128)(2,1)} async-done(((bf16[12,2,256,256]{3,0,1,2:T(8,128)(2,1)}), bf16[12,2,256,256]{3,0,1,2:T(8,128)(2,1)}, u32[]{:S(2)}, u32[]{:S(2)}) %all-to-all-start) | async-done | bytes 3145760 | tf_op jit(solution)/shard_map/all_to_all | solution.py:34
  401.5 5.6 %copy.38 = bf16[12,2,256,256]{3,2,1,0:T(8,128)(2,1)} copy(bf16[12,2,256,256]{3,0,1,2:T(8,128)(2,1)} %all-to-all-done) | data formatting | bytes 6291456
  407.1 4.3 %copy.37 = bf16[12,2,256,256]{3,2,1,0:T(8,128)(2,1)} copy(bf16[12,2,256,256]{3,1,0,2:T(2,128)(2,1)} %all-gather.2.cloned.1.call-done) | data formatting | bytes 6291456
  (45 shorter events, 18.1 us)
Async XLA Ops:
  7.2 158.9 %reduce-scatter.2.cloned.1.call-start = ((), (), s32[]{:S(2)}) async-start(), calls=%async_computation.2 | async-start | bytes 8519680 | tf_op jit(solution)/shard_map/reduce_scatter | solution.py:20
  14.2 232.9 %copy-start = (f32[12,2,4,256]{3,2,1,0:T(4,128)S(1)}, f32[12,2,4,256]{3,2,1,0:T(4,128)}, u32[]{:S(2)}) copy-start(f32[12,2,4,256]{3,2,1,0:T(4,128)} %param.8) | copy-start | bytes 294916
  14.2 232.9 %copy-start.1 = (f32[12,2,4,256]{3,2,1,0:T(4,128)S(1)}, f32[12,2,4,256]{3,2,1,0:T(4,128)}, u32[]{:S(2)}) copy-start(f32[12,2,4,256]{3,2,1,0:T(4,128)} %param.7) | copy-start | bytes 294916
  14.2 232.9 %copy-start.2 = (f32[12,2,4,256]{3,2,1,0:T(4,128)S(1)}, f32[12,2,4,256]{3,2,1,0:T(4,128)}, u32[]{:S(2)}) copy-start(f32[12,2,4,256]{3,2,1,0:T(4,128)} %param.9) | copy-start | bytes 294916
  14.2 232.9 %copy-start.3 = (f32[12,2,4,256]{3,2,1,0:T(4,128)S(1)}, f32[12,2,4,256]{3,2,1,0:T(4,128)}, u32[]{:S(2)}) copy-start(f32[12,2,4,256]{3,2,1,0:T(4,128)} %param.10) | copy-start | bytes 294916
  14.2 232.9 %copy-start.4 = (f32[12]{0:T(128)S(1)}, f32[12]{0:T(128)}, u32[]{:S(2)}) copy-start(f32[12]{0:T(128)} %param.11) | copy-start | bytes 148
  288.2 113.3 %all-to-all-start = ((bf16[12,2,256,256]{3,0,1,2:T(8,128)(2,1)}), bf16[12,2,256,256]{3,0,1,2:T(8,128)(2,1)}, u32[]{:S(2)}, u32[]{:S(2)}) async-start(bf16[12,2,256,256]{3,0,1,2:T(8,128)(2,1)} %constant_dynamic-update-slice_fusion), calls=%async_computation.1 | async-start | bytes 8388608 | tf_op jit(solution)/shard_map/all_to_all | solution.py:34
  296.0 111.1 %all-gather.2.cloned.1.call-start = ((), (), s32[]{:S(2)}) async-start(), calls=%async_computation.3 | async-start | bytes 3194880 | tf_op jit(solution)/shard_map/all_gather | solution.py:31
Sparse Core Ops, SparseCore 0:
  14.4 151.6 reduce-scatter.1
  300.2 96.6 all-gather.1

commit v2 on v0

--- a/solution.py
+++ b/solution.py
@@ -2,6 +2,7 @@
 import jax.numpy as jnp
 from jax import lax
 from jax.sharding import PartitionSpec as P
+from jax.lax import all_to_all, axis_size
 
 OWN = ("dp", "fsdp")
 ALL = ("dp", "fsdp", "mp")
@@ -28,7 +29,12 @@
     layer_rate = layer_rates[:, None, None, None]
     master_new = master - layer_rate * direction
     teacher_new = EMA_KEEP * teacher + (1.0 - EMA_KEEP) * master_new
-    student = lax.all_gather(master_new.astype(jnp.bfloat16), OWN, axis=2, tiled=True)
+    student = jnp.concatenate(
+        all_to_all(
+            jnp.stack([master_new.astype(jnp.bfloat16)] * axis_size(OWN), axis=0), OWN, 0, 0
+        ),
+        2,
+    )
     teach = lax.all_gather(teacher_new.astype(jnp.bfloat16), OWN, axis=2, tiled=True)
     return (master_new, teacher_new, first_new, second_new, student, teach)
 

time: 413 us -> 361 us (0.87)
  waiting for transfers between devices: 297 us -> 230 us
  starting transfers between devices: 0.12 us -> 7.65 us
  local copies, waits for them, and re-layouts: 12.7 us -> 18.2 us
    all_to_all x0 -> x1, waiting for transfers between devices: none -> 74.4 us  [shards(): all_to_all(jnp.stack([master_new.astype(jnp.bfloat16)] * axis_size(OWN),...]
    all_gather x1 -> x0, waiting for transfers between devices: 71.5 us -> none  [shards(): lax.all_gather(master_new.astype(jnp.bfloat16), OWN, axis=2, tiled=True)]
    all_gather x1, waiting for transfers between devices: 73.9 us -> 4.22 us  [shards(): lax.all_gather(teacher_new.astype(jnp.bfloat16), OWN, axis=2, tiled=True)]
    all_to_all x0 -> x1, starting transfers between devices: none -> 7.58 us  [shards(): all_to_all(jnp.stack([master_new.astype(jnp.bfloat16)] * axis_size(OWN),...]
  transfers between devices with their start and end apart: 3 -> 3, of which waited for: 3 -> 3; matrix products, arithmetic and copies ran while one was open for 2% -> 3% of each run, Pallas kernels for 0% -> 0%
where the time goes in v2:
time: 361 us; the launch traced here: 360 us
  waiting for transfers between devices  230 us (64%)
  blocking collectives  78.7 us (22%)
  local copies, waits for them, and re-layouts  18.2 us (5%)
  between operations  14.9 us (4%)
  other arithmetic  10.4 us (3%)
  starting transfers between devices  7.65 us (2%)
    reduce_scatter x1, waiting for transfers between devices, shards(): summed = lax.psum_scatter(own_grad, OWN, scatter_dimension=2, tiled=True)  152 us
    psum x1, blocking collectives, shards(): norm_sq = lax.psum(jnp.sum(mean_grad * mean_grad), ALL)  78.7 us
    all_to_all x1, waiting for transfers between devices, shards(): all_to_all(jnp.stack([master_new.astype(jnp.bfloat16)] * axis_size(OWN),...  74.4 us
    unnamed x16, local copies, waits for them, and re-layouts  10.3 us
    all_to_all x1, starting transfers between devices, shards(): all_to_all(jnp.stack([master_new.astype(jnp.bfloat16)] * axis_size(OWN),...  7.58 us
  transfers between devices with their start and end apart: 3, of which 3 were waited for; matrix products, arithmetic and copies ran while one was open for 3% of the time, Pallas kernels for 0%

profile of v2, /device:TPU:1, one launch (start us, length us, event | category | flops | bytes accessed | tf_op | source)
XLA Modules:
  0.0 360.3 jit_solution(17079457311985119159)
XLA Ops:
  7.2 0.0 reduce-scatter.2.cloned.1.call-start
  7.2 7.0 %bitcast_convert_fusion = f32[12,2,256,256]{3,0,1,2:T(8,128)} fusion(bf16[1,12,2,256,256]{4,3,2,1,0:T(8,128)(2,1)} %param.6), kind=kLoop, calls=%fused_computation | loop fusion | flops 1572864 | bytes 9437184 | tf_op jit(solution)/shard_map/convert_element_type | solution.py:20
  14.2 0.0 copy-start
  14.2 0.0 copy-start.1
  14.2 0.0 copy-start.2
  14.2 0.0 copy-start.3
  14.2 0.0 copy-start.4
  14.2 0.0 reduce-scatter.2.cloned.1.call-update
  14.3 151.8 %reduce-scatter.2.cloned.1.call-done = f32[12,2,4,256]{3,0,1,2:T(8,128)} async-done(((f32[12,2,256,256]{3,0,1,2:T(8,128)}), f32[12,2,4,256]{3,0,1,2:T(8,128)}) %reduce-scatter.2.cloned.1.call-update) | async-done | bytes 98320 | tf_op jit(solution)/shard_map/reduce_scatter | solution.py:21
  166.1 1.5 multiply_reduce_fusion
  167.6 78.7 %psum.7 = f32[]{:T(128)} all-reduce(f32[]{:T(128)} %multiply_reduce_fusion), channel_id=1, replica_groups=mesh['dp'=8,'fsdp'=8,'mp'=4] {'dp','fsdp','mp'}, use_global_device_ids=true, to_apply=%region_2.0 | all-reduce | flops 1 | bytes 8 | tf_op jit(solution)/shard_map/psum | solution.py:23
  247.1 0.0 copy-done
  247.1 0.0 copy-done.1
  247.1 0.0 copy-done.2
  247.1 0.0 copy-done.3
  247.1 0.0 copy-done.4
  247.1 1.8 fusion.5
  249.0 3.2 stack.2
  252.2 7.6 %all-to-all-start = ((bf16[64,12,2,4,256]{4,3,2,1,0:T(4,128)(2,1)}), bf16[64,12,2,4,256]{4,3,2,1,0:T(4,128)(2,1)S(1)}, u32[]{:S(2)}, u32[]{:S(2)}) async-start(bf16[64,12,2,4,256]{4,3,2,1,0:T(4,128)(2,1)} %stack.2), calls=%async_computation.1 | async-start | bytes 6291456 | tf_op jit(solution)/shard_map/all_to_all | solution.py:33
  259.8 0.0 all-gather.2.cloned.1.call-start
  259.8 1.5 copy.33
  261.3 0.0 all-gather.2.cloned.1.call-update
  261.3 0.7 copy.34
  262.0 1.6 copy.35
  263.6 0.7 copy.36
  264.3 0.7 copy.37
  265.1 74.4 %all-to-all-done = bf16[64,12,2,4,256]{4,3,2,1,0:T(4,128)(2,1)S(1)} async-done(((bf16[64,12,2,4,256]{4,3,2,1,0:T(4,128)(2,1)}), bf16[64,12,2,4,256]{4,3,2,1,0:T(4,128)(2,1)S(1)}, u32[]{:S(2)}, u32[]{:S(2)}) %all-to-all-start) | async-done | bytes 3145760 | tf_op jit(solution)/shard_map/all_to_all | solution.py:33
  339.5 3.2 copy.32
  342.7 2.2 copy.38
  344.9 4.2 %all-gather.2.cloned.1.call-done = bf16[12,2,256,256]{3,1,0,2:T(2,128)(2,1)} async-done(((bf16[12,2,4,256]{3,1,0,2:T(2,128)(2,1)}), bf16[12,2,256,256]{3,1,0,2:T(2,128)(2,1)}) %all-gather.2.cloned.1.call-update) | async-done | bytes 3145744 | tf_op jit(solution)/shard_map/all_gather | solution.py:38
  349.2 4.3 %copy.39 = bf16[12,2,256,256]{3,2,1,0:T(8,128)(2,1)} copy(bf16[12,2,256,256]{3,1,0,2:T(2,128)(2,1)} %all-gather.2.cloned.1.call-done) | data formatting | bytes 6291456
  (2 shorter events, 0.1 us)
Async XLA Ops:
  7.2 158.9 %reduce-scatter.2.cloned.1.call-start = ((), (), s32[]{:S(2)}) async-start(), calls=%async_computation.2 | async-start | bytes 8519680 | tf_op jit(solution)/shard_map/reduce_scatter | solution.py:21
  14.2 232.9 %copy-start = (f32[12,2,4,256]{3,2,1,0:T(4,128)S(1)}, f32[12,2,4,256]{3,2,1,0:T(4,128)}, u32[]{:S(2)}) copy-start(f32[12,2,4,256]{3,2,1,0:T(4,128)} %param.8) | copy-start | bytes 294916
  14.2 232.9 %copy-start.1 = (f32[12,2,4,256]{3,2,1,0:T(4,128)S(1)}, f32[12,2,4,256]{3,2,1,0:T(4,128)}, u32[]{:S(2)}) copy-start(f32[12,2,4,256]{3,2,1,0:T(4,128)} %param.7) | copy-start | bytes 294916
  14.2 232.9 %copy-start.2 = (f32[12,2,4,256]{3,2,1,0:T(4,128)S(1)}, f32[12,2,4,256]{3,2,1,0:T(4,128)}, u32[]{:S(2)}) copy-start(f32[12,2,4,256]{3,2,1,0:T(4,128)} %param.9) | copy-start | bytes 294916
  14.2 232.9 %copy-start.3 = (f32[12,2,4,256]{3,2,1,0:T(4,128)S(1)}, f32[12,2,4,256]{3,2,1,0:T(4,128)}, u32[]{:S(2)}) copy-start(f32[12,2,4,256]{3,2,1,0:T(4,128)} %param.10) | copy-start | bytes 294916
  14.2 232.9 %copy-start.4 = (f32[12]{0:T(128)S(1)}, f32[12]{0:T(128)}, u32[]{:S(2)}) copy-start(f32[12]{0:T(128)} %param.11) | copy-start | bytes 148
  252.2 87.3 %all-to-all-start = ((bf16[64,12,2,4,256]{4,3,2,1,0:T(4,128)(2,1)}), bf16[64,12,2,4,256]{4,3,2,1,0:T(4,128)(2,1)S(1)}, u32[]{:S(2)}, u32[]{:S(2)}) async-start(bf16[64,12,2,4,256]{4,3,2,1,0:T(4,128)(2,1)} %stack.2), calls=%async_computation.1 | async-start | bytes 6291456 | tf_op jit(solution)/shard_map/all_to_all | solution.py:33
  259.8 89.4 %all-gather.2.cloned.1.call-start = ((), (), s32[]{:S(2)}) async-start(), calls=%async_computation.3 | async-start | bytes 3194880 | tf_op jit(solution)/shard_map/all_gather | solution.py:38
Sparse Core Ops, SparseCore 0:
  14.4 151.6 reduce-scatter.1
  263.3 85.7 all-gather.1
